TPU v7x, 32 devices: a whole 2x2x4 slice. The times are simulated.
32 devices in a mesh: freq: 32 (over z, y, x, core).
Axes of the slice: x: 2, y: 2, z: 4, core: 2. Of those that a mesh axis runs over, the one named last changes fastest.
Arguments:
- pulses: float32 [1, 2, 30, 65536], P(None, None, None, 'freq'), may hold values from -4 to 4
- coupling: float32 [2, 30, 30, 65536], P(None, None, None, 'freq'), may hold values from -0.4 to 0.4
- dispersion_terms: float32 [3, 30], replicated, may hold values from -3 to 3
- kerr_gain: float32 [30], replicated, may hold values from 0.01 to 0.08
Outputs:
- evolved: float32 [1, 2, 30, 65536], P(None, None, None, 'freq')
All inputs are finite; a program needn't handle non-finite values.
Results may differ from a plain program's by a relative error of at most 0.00027.
Values sent between devices are 32-bit elements; how exact they have to be, the bound alone decides.
A program may use at most 128 MiB of HBM per device.

v0:
```python
import jax
import jax.numpy as jnp
from jax import lax
from jax.sharding import PartitionSpec as P

STEPS = 2
HIGHEST = lax.Precision.HIGHEST


def angle_table(first, second, modulus, orient):
    turns = first[:, None] * second[None, :] % modulus
    radians = turns.astype(jnp.float32) * (2.0 * jnp.pi / modulus)
    return (jnp.cos(radians), orient * jnp.sin(radians))


def rotate(real_part, imag_part, cosine, sine):
    return (real_part * cosine - imag_part * sine, real_part * sine + imag_part * cosine)


def transform(stacked, cosine, sine):
    real_part = stacked[:, 0]
    imag_part = stacked[:, 1]
    out_real = jnp.matmul(real_part, cosine, precision=HIGHEST) - jnp.matmul(
        imag_part, sine, precision=HIGHEST
    )
    out_imag = jnp.matmul(real_part, sine, precision=HIGHEST) + jnp.matmul(
        imag_part, cosine, precision=HIGHEST
    )
    return jnp.stack((out_real, out_imag), axis=1)


def nonlinear_phase(stacked, kerr_gain):
    magnitude = stacked[:, 0] ** 2 + stacked[:, 1] ** 2
    total_power = jnp.sum(magnitude, axis=1, keepdims=True)
    gains = kerr_gain.reshape((1, -1) + (1,) * (magnitude.ndim - 2))
    angles = gains * (2.0 * total_power - magnitude)
    real_part, imag_part = rotate(stacked[:, 0], stacked[:, 1], jnp.cos(angles), jnp.sin(angles))
    return jnp.stack((real_part, imag_part), axis=1)


def per_device(pulses, coupling, dispersion_terms, kerr_gain):
    shards = lax.axis_size("freq")
    device = lax.axis_index("freq")
    mode_count = pulses.shape[2]
    local_count = pulses.shape[3]
    groups = local_count // shards
    total_count = local_count * shards
    column_index = jnp.arange(shards, dtype=jnp.int32)
    row_index = jnp.arange(local_count, dtype=jnp.int32)
    short_cos, short_sin = angle_table(column_index, column_index, shards, -1.0)
    inverse_short_cos, inverse_short_sin = angle_table(column_index, column_index, shards, 1.0)
    long_cos, long_sin = angle_table(row_index, row_index, local_count, -1.0)
    inverse_long_cos, inverse_long_sin = angle_table(row_index, row_index, local_count, 1.0)
    sample_rows = jnp.arange(groups, dtype=jnp.int32) * shards + device
    twist_cos, twist_sin = angle_table(sample_rows, column_index, total_count, -1.0)
    untwist_cos, untwist_sin = angle_table(row_index, jnp.reshape(device, (1,)), total_count, 1.0)
    untwist_cos = untwist_cos.reshape(-1)
    untwist_sin = untwist_sin.reshape(-1)
    bins = device + shards * row_index
    signed_bin = jnp.where(bins < total_count // 2, bins, bins - total_count).astype(jnp.float32)
    angular = signed_bin / (total_count // 2)
    dispersion = (
        dispersion_terms[0][:, None] * angular
        + dispersion_terms[1][:, None] * angular**2 / 2
        + dispersion_terms[2][:, None] * angular**3 / 6
    )
    spread_cos = jnp.cos(dispersion)
    spread_sin = jnp.sin(dispersion)
    identity = jnp.eye(mode_count, dtype=jnp.float32)[:, :, None]
    mixing_real = coupling[0] + identity
    mixing_imag = coupling[1]
    blocks = pulses.reshape(pulses.shape[0], 2, mode_count, groups, shards)
    columns = lax.all_to_all(blocks, "freq", split_axis=4, concat_axis=4, tiled=True)
    for repeat in range(STEPS):
        spectral = transform(columns, short_cos, short_sin)
        forward_real_part, forward_imag_part = rotate(
            spectral[:, 0], spectral[:, 1], twist_cos, twist_sin
        )
        evolve_rows = lax.all_to_all(
            jnp.stack((forward_real_part, forward_imag_part), axis=1),
            "freq",
            split_axis=4,
            concat_axis=4,
            tiled=True,
        )
        flat = evolve_rows.reshape(evolve_rows.shape[0], 2, mode_count, local_count)
        spectrum = transform(flat, long_cos, long_sin)
        spec_real = spectrum[:, 0]
        spec_imag = spectrum[:, 1]
        mixed_real = jnp.einsum(
            "nmk,bmk->bnk", mixing_real, spec_real, precision=HIGHEST
        ) - jnp.einsum("nmk,bmk->bnk", mixing_imag, spec_imag, precision=HIGHEST)
        mixed_imag = jnp.einsum(
            "nmk,bmk->bnk", mixing_real, spec_imag, precision=HIGHEST
        ) + jnp.einsum("nmk,bmk->bnk", mixing_imag, spec_real, precision=HIGHEST)
        real_part, imag_part = rotate(mixed_real, mixed_imag, spread_cos, spread_sin)
        inverted = transform(
            jnp.stack((real_part, imag_part), axis=1), inverse_long_cos, inverse_long_sin
        )
        real_part, imag_part = rotate(inverted[:, 0], inverted[:, 1], untwist_cos, untwist_sin)
        moved = jnp.stack((real_part, imag_part), axis=1).reshape(evolve_rows.shape)
        columns = nonlinear_phase(
            transform(
                lax.all_to_all(moved, "freq", split_axis=4, concat_axis=4, tiled=True),
                inverse_short_cos,
                inverse_short_sin,
            )
            * (1.0 / total_count),
            kerr_gain,
        )
    returned = lax.all_to_all(columns, "freq", split_axis=4, concat_axis=4, tiled=True)
    return returned.reshape(columns.shape[0], 2, mode_count, local_count)


def solution(mesh):
    in_specs = (P(None, None, None, "freq"), P(None, None, None, "freq"), P(), P())
    out_specs = P(None, None, None, "freq")
    return jax.shard_map(
        per_device, mesh=mesh, in_specs=in_specs, out_specs=out_specs, check_vma=False
    )
```

profile of v0, /device:TPU:0, one launch (start us, length us, event | category | flops | bytes accessed | tf_op | source)
XLA Modules:
  0.0 1394.7 jit_solution(16185330490249208704)
XLA Ops:
  0.0 1.9 reshape.856
  1.9 0.9 copy.36
  2.8 1.8 reshape.893
  4.6 7.3 all-to-all-start
  12.1 14.9 %all-to-all-done = f32[32,1,3840]{2,1,0:T(1,128)S(1)} async-done(((f32[32,1,3840]{2,1,0:T(1,128)}), f32[32,1,3840]{2,1,0:T(1,128)S(1)}, u32[]{:S(2)}, u32[]{:S(2)}) %all-to-all-start) | async-done | bytes 491552 | tf_op jit(solution)/shard_map/all_to_all | solution.py:73
  27.6 1.8 reduce.20
  33.6 0.8 copy.207
  34.3 1.8 reshape.895
  36.1 3.1 all-to-all-start.1
  39.2 19.7 %fusion.344 = (f32[1,30,30,2048]{3,0,2,1:T(1,128)}, f32[1,30,30,2048]{3,0,2,1:T(1,128)}) fusion(f32[2,30,30,2048]{3,0,2,1:T(2,128)} %param.5), kind=kLoop, calls=%fused_computation.366 | loop fusion | bytes 29491200 | tf_op jit(solution)/shard_map/slice | solution.py:70
  60.3 1.8 reduce.21
  62.8 0.8 copy.40
  63.6 1.1 reshape.859
  65.1 71.2 %fusion.12 = f32[30,2048]{1,0:T(8,128)S(1)} fusion(f32[1,1,30,2048]{3,1,2,0:T(1,128)S(1)} %get-tuple-element.41), kind=kOutput, calls=%fused_computation.15 | convolution fusion | flops 1572864000 | bytes 491520 | tf_op jit(solution)/shard_map/dot_general | solution.py:23
  136.3 71.4 %fusion.10 = f32[30,2048]{1,0:T(8,128)S(1)} fusion(f32[1,1,30,2048]{3,1,2,0:T(1,128)S(1)} %get-tuple-element.42), kind=kOutput, calls=%fused_computation.13 | convolution fusion | flops 1572864000 | bytes 491520 | tf_op jit(solution)/shard_map/dot_general | solution.py:26
  207.7 70.6 %fusion.65 = f32[2048,30]{0,1:T(8,128)S(1)} fusion(f32[30,2048]{1,0:T(8,128)S(1)} %fusion.12, f32[1,1,30,2048]{3,1,2,0:T(1,128)S(1)} %get-tuple-element.42), kind=kOutput, calls=%fused_computation.52 | convolution fusion | flops 1568731136 | bytes 737280 | tf_op jit(solution)/shard_map/dot_general | solution.py:23
  278.4 70.4 %fusion.71 = f32[2048,30]{0,1:T(8,128)S(1)} fusion(f32[30,2048]{1,0:T(8,128)S(1)} %fusion.10, f32[1,1,30,2048]{3,1,2,0:T(1,128)S(1)} %get-tuple-element.41), kind=kOutput, calls=%fused_computation.54 | convolution fusion | flops 1568731136 | bytes 737280 | tf_op jit(solution)/shard_map/dot_general | solution.py:26
  348.8 11.7 multiply_reduce_fusion.6
  361.2 1.3 copy.73
  362.5 1.4 copy.80
  364.0 6.9 fusion.100
  370.8 74.2 %fusion.30 = f32[30,2048]{1,0:T(8,128)S(1)} fusion(f32[30,2048]{0,1:T(8,128)S(1)} %get-tuple-element.21), kind=kOutput, calls=%fused_computation.28 | convolution fusion | flops 1568669696 | bytes 491520 | tf_op jit(solution)/shard_map/dot_general | solution.py:23
  445.1 74.4 %fusion.28 = f32[30,2048]{1,0:T(8,128)S(1)} fusion(f32[1,30,2048]{1,2,0:T(8,128)S(1)} %get-tuple-element.22), kind=kOutput, calls=%fused_computation.27 | convolution fusion | flops 1568669696 | bytes 491520 | tf_op jit(solution)/shard_map/dot_general | solution.py:26
  519.5 74.7 %fusion.50 = f32[30,2048]{1,0:T(8,128)S(1)} fusion(f32[30,2048]{1,0:T(8,128)S(1)} %fusion.30, f32[1,30,2048]{1,2,0:T(8,128)S(1)} %get-tuple-element.22), kind=kOutput, calls=%fused_computation.47 | convolution fusion | flops 1568731136 | bytes 737280 | tf_op jit(solution)/shard_map/dot_general | solution.py:23
  594.3 75.0 %multiply_subtract_fusion.2 = (f32[30,2048]{1,0:T(8,128)S(1)}, f32[30,2048]{1,0:T(8,128)S(1)}) fusion(f32[30,2048]{1,0:T(8,128)S(1)} %fusion.50, f32[2048]{0:T(1024)S(1)} %copy-done.12, f32[2048]{0:T(1024)S(1)} %copy-done.14, f32[30,2048]{1,0:T(8,128)S(1)} %fusion.28, f32[30,2048]{0,1:T(8,128)S(1)} %get-tuple-element.21), kind=kOutput, calls=%fused_computation.146 | convolution fusion | flops 1569099776 | bytes 1245184 | tf_op jit(solution)/shard_map/dot_general | solution.py:26
  669.6 1.3 stack.63
  670.9 1.4 pad_maximum_fusion
  672.3 0.9 copy.43
  673.3 1.0 reshape.897
  674.3 20.9 %all_to_all.30 = f32[32,1,3840]{2,1,0:T(1,128)S(1)} all-to-all(f32[32,1,3840]{2,1,0:T(1,128)S(1)} %reshape.897), channel_id=1, replica_groups=mesh['freq'=32] {'freq'}, dimensions={0} | all-to-all | bytes 983040 | tf_op jit(solution)/shard_map/all_to_all | solution.py:104
  695.2 1.8 reduce.22
  701.3 2.1 fusion.107
  704.7 2.5 convolution_add_fusion.1
  707.3 2.6 subtract_bitcast_fusion
  709.9 0.8 copy.206
  710.7 1.0 reshape.899
  711.8 17.7 %all_to_all.31 = f32[32,1,3840]{2,1,0:T(1,128)S(1)} all-to-all(f32[32,1,3840]{2,1,0:T(1,128)S(1)} %reshape.899), channel_id=1, replica_groups=mesh['freq'=32] {'freq'}, dimensions={0} | all-to-all | bytes 983040 | tf_op jit(solution)/shard_map/all_to_all | solution.py:79
  729.4 1.8 reduce.23
  732.0 0.8 copy.47
  732.8 1.1 reshape.866
  734.2 71.6 %fusion.8 = f32[30,2048]{1,0:T(8,128)S(1)} fusion(f32[1,1,30,2048]{3,1,2,0:T(1,128)S(1)} %get-tuple-element.39), kind=kOutput, calls=%fused_computation.11 | convolution fusion | flops 1572864000 | bytes 491520 | tf_op jit(solution)/shard_map/dot_general | solution.py:23
  805.9 71.4 %fusion.6 = f32[30,2048]{1,0:T(8,128)S(1)} fusion(f32[1,1,30,2048]{3,1,2,0:T(1,128)S(1)} %get-tuple-element.40), kind=kOutput, calls=%fused_computation.9 | convolution fusion | flops 1572864000 | bytes 491520 | tf_op jit(solution)/shard_map/dot_general | solution.py:26
  877.3 70.4 %fusion.77 = f32[2048,30]{0,1:T(8,128)S(1)} fusion(f32[30,2048]{1,0:T(8,128)S(1)} %fusion.8, f32[1,1,30,2048]{3,1,2,0:T(1,128)S(1)} %get-tuple-element.40), kind=kOutput, calls=%fused_computation.56 | convolution fusion | flops 1568731136 | bytes 737280 | tf_op jit(solution)/shard_map/dot_general | solution.py:23
  947.7 70.6 %fusion.83 = f32[2048,30]{0,1:T(8,128)S(1)} fusion(f32[30,2048]{1,0:T(8,128)S(1)} %fusion.6, f32[1,1,30,2048]{3,1,2,0:T(1,128)S(1)} %get-tuple-element.39), kind=kOutput, calls=%fused_computation.58 | convolution fusion | flops 1568731136 | bytes 737280 | tf_op jit(solution)/shard_map/dot_general | solution.py:26
  1018.4 11.7 multiply_reduce_fusion.2
  1030.8 1.3 copy.87
  1032.1 1.3 copy.94
  1033.5 6.9 fusion.95
  1040.4 74.2 %fusion.22 = f32[30,2048]{1,0:T(8,128)S(1)} fusion(f32[30,2048]{0,1:T(8,128)S(1)} %get-tuple-element.19), kind=kOutput, calls=%fused_computation.24 | convolution fusion | flops 1568669696 | bytes 491520 | tf_op jit(solution)/shard_map/dot_general | solution.py:23
  1114.6 74.2 %fusion.20 = f32[30,2048]{1,0:T(8,128)S(1)} fusion(f32[1,30,2048]{1,2,0:T(8,128)S(1)} %get-tuple-element.20), kind=kOutput, calls=%fused_computation.23 | convolution fusion | flops 1568669696 | bytes 491520 | tf_op jit(solution)/shard_map/dot_general | solution.py:26
  1188.9 75.0 %fusion.56 = f32[30,2048]{1,0:T(8,128)S(1)} fusion(f32[30,2048]{1,0:T(8,128)S(1)} %fusion.22, f32[1,30,2048]{1,2,0:T(8,128)S(1)} %get-tuple-element.20), kind=kOutput, calls=%fused_computation.49 | convolution fusion | flops 1568731136 | bytes 737280 | tf_op jit(solution)/shard_map/dot_general | solution.py:23
  1263.9 74.8 %multiply_subtract_fusion.1 = (f32[30,2048]{1,0:T(8,128)S(1)}, f32[30,2048]{1,0:T(8,128)S(1)}) fusion(f32[30,2048]{1,0:T(8,128)S(1)} %fusion.56, f32[2048]{0:T(1024)S(1)} %copy-done.13, f32[2048]{0:T(1024)S(1)} %copy-done.15, f32[30,2048]{1,0:T(8,128)S(1)} %fusion.20, f32[30,2048]{0,1:T(8,128)S(1)} %get-tuple-element.19), kind=kOutput, calls=%fused_computation.144 | convolution fusion | flops 1569099776 | bytes 1245184 | tf_op jit(solution)/shard_map/dot_general | solution.py:26
  1339.0 1.3 stack.72
  1340.2 1.4 pad_maximum_fusion.1
  1341.6 0.9 copy.48
  1342.6 1.0 reshape.901
  1343.6 17.9 %all_to_all.32 = f32[32,1,3840]{2,1,0:T(1,128)S(1)} all-to-all(f32[32,1,3840]{2,1,0:T(1,128)S(1)} %reshape.901), channel_id=1, replica_groups=mesh['freq'=32] {'freq'}, dimensions={0} | all-to-all | bytes 983040 | tf_op jit(solution)/shard_map/all_to_all | solution.py:104
  1361.5 1.8 reduce.24
  1367.6 2.1 multiply_subtract_fusion
  1370.6 1.0 reshape.903
  1371.6 17.7 %all_to_all.33 = f32[32,1,3840]{2,1,0:T(1,128)S(1)} all-to-all(f32[32,1,3840]{2,1,0:T(1,128)S(1)} %reshape.903), channel_id=1, replica_groups=mesh['freq'=32] {'freq'}, dimensions={0} | all-to-all | bytes 983040 | tf_op jit(solution)/shard_map/all_to_all | solution.py:111
  1389.3 1.8 reduce.25
  1391.8 0.8 copy.52
  1392.7 1.8 reshape.873
  (120 shorter events, 21.6 us)
Async XLA Ops:
  4.6 22.4 %all-to-all-start = ((f32[32,1,3840]{2,1,0:T(1,128)}), f32[32,1,3840]{2,1,0:T(1,128)S(1)}, u32[]{:S(2)}, u32[]{:S(2)}) async-start(f32[32,1,3840]{2,1,0:T(1,128)} %reshape.893), calls=%async_computation | async-start | bytes 983040 | tf_op jit(solution)/shard_map/all_to_all | solution.py:73
  12.1 46.8 %copy-start = (f32[64,32]{0,1:T(8,128)}, f32[64,32]{0,1:T(8,128)S(1)}, u32[]{:S(2)}) copy-start(f32[64,32]{0,1:T(8,128)S(1)} %get-tuple-element.46) | copy-start | bytes 24580
  12.1 46.8 %copy-start.2 = (f32[64,32]{0,1:T(8,128)}, f32[64,32]{0,1:T(8,128)S(1)}, u32[]{:S(2)}) copy-start(f32[64,32]{0,1:T(8,128)S(1)} %get-tuple-element.47) | copy-start | bytes 24580
  36.1 24.2 %all-to-all-start.1 = ((f32[32,1,3840]{2,1,0:T(1,128)}), f32[32,1,3840]{2,1,0:T(1,128)S(1)}, u32[]{:S(2)}, u32[]{:S(2)}) async-start(f32[32,1,3840]{2,1,0:T(1,128)} %reshape.895), calls=%async_computation.1 | async-start | bytes 983040 | tf_op jit(solution)/shard_map/all_to_all | solution.py:79
  39.2 21.0 %copy-start.24 = (f32[3,30]{1,0:T(4,128)S(1)}, f32[3,30]{1,0:T(4,128)}, u32[]{:S(2)}) copy-start(f32[3,30]{1,0:T(4,128)} %param.6) | copy-start | bytes 1084
  58.9 305.0 %copy-start.6 = (f32[2048]{0:T(1024)}, f32[2048]{0:T(1024)S(1)}, u32[]{:S(2)}) copy-start(f32[2048]{0:T(1024)S(1)} %fusion.202) | copy-start | bytes 24580
  58.9 289.8 %copy-start.4 = (f32[30,30]{1,0:T(8,128)}, f32[30,30]{1,0:T(8,128)S(1)}, u32[]{:S(2)}) copy-start(f32[30,30]{1,0:T(8,128)S(1)} %fusion.163) | copy-start | bytes 10804
  59.6 304.3 %copy-start.8 = (f32[2048]{0:T(1024)}, f32[2048]{0:T(1024)S(1)}, u32[]{:S(2)}) copy-start(f32[2048]{0:T(1024)S(1)} %get-tuple-element.48) | copy-start | bytes 24580
  60.3 303.7 %copy-start.10 = (f32[2048]{0:T(1024)}, f32[2048]{0:T(1024)S(1)}, u32[]{:S(2)}) copy-start(f32[2048]{0:T(1024)S(1)} %get-tuple-element.51) | copy-start | bytes 24580
  60.3 303.7 %copy-start.16 = (f32[30]{0:T(128)}, f32[30]{0:T(128)S(1)}, u32[]{:S(2)}) copy-start(f32[30]{0:T(128)S(1)} %get-tuple-element.43) | copy-start | bytes 364
  60.3 303.6 %copy-start.18 = (f32[30]{0:T(128)}, f32[30]{0:T(128)S(1)}, u32[]{:S(2)}) copy-start(f32[30]{0:T(128)S(1)} %get-tuple-element.44) | copy-start | bytes 364
  60.3 303.6 %copy-start.20 = (f32[30]{0:T(128)}, f32[30]{0:T(128)S(1)}, u32[]{:S(2)}) copy-start(f32[30]{0:T(128)S(1)} %get-tuple-element.45) | copy-start | bytes 364
  207.7 141.0 %slice-start = ((s8[7372800]{0:T(1024)(128)(4,1)}), s8[4194304]{0:T(1024)(128)(4,1)S(1)}, s32[]{:S(2)}) async-start(s8[7372800]{0:T(1024)(128)(4,1)} %bitcast.327), calls=%async_computation.6 | async-start | bytes 8388608
  207.7 141.0 %slice-start.4 = ((s8[7372800]{0:T(1024)(128)(4,1)}), s8[4194304]{0:T(1024)(128)(4,1)S(1)}, s32[]{:S(2)}) async-start(s8[7372800]{0:T(1024)(128)(4,1)} %bitcast.331), calls=%async_computation.10 | async-start | bytes 8388608
  278.3 70.4 %slice-start.1 = ((s8[7372800]{0:T(1024)(128)(4,1)}), s8[3178496]{0:T(1024)(128)(4,1)S(1)}, s32[]{:S(2)}) async-start(s8[7372800]{0:T(1024)(128)(4,1)} %bitcast.327), calls=%async_computation.7 | async-start | bytes 6356992
  278.4 70.4 %slice-start.5 = ((s8[7372800]{0:T(1024)(128)(4,1)}), s8[3178496]{0:T(1024)(128)(4,1)S(1)}, s32[]{:S(2)}) async-start(s8[7372800]{0:T(1024)(128)(4,1)} %bitcast.331), calls=%async_computation.11 | async-start | bytes 6356992
  519.5 74.8 %copy-start.12 = (f32[2048]{0:T(1024)S(1)}, f32[2048]{0:T(1024)}, u32[]{:S(2)}) copy-start(f32[2048]{0:T(1024)} %get-tuple-element.49) | copy-start | bytes 24580
  519.5 74.8 %copy-start.14 = (f32[2048]{0:T(1024)S(1)}, f32[2048]{0:T(1024)}, u32[]{:S(2)}) copy-start(f32[2048]{0:T(1024)} %get-tuple-element.50) | copy-start | bytes 24580
  669.3 32.0 %copy-start.22 = (f32[30]{0:T(128)S(1)}, f32[30]{0:T(128)}, u32[]{:S(2)}) copy-start(f32[30]{0:T(128)} %param.7) | copy-start | bytes 364
  669.3 37.9 %copy-start.1 = (f32[64,32]{0,1:T(8,128)S(1)}, f32[64,32]{0,1:T(8,128)}, u32[]{:S(2)}) copy-start(f32[64,32]{0,1:T(8,128)} %copy-done) | copy-start | bytes 24580
  669.3 37.9 %copy-start.3 = (f32[64,32]{0,1:T(8,128)S(1)}, f32[64,32]{0,1:T(8,128)}, u32[]{:S(2)}) copy-start(f32[64,32]{0,1:T(8,128)} %copy-done.2) | copy-start | bytes 24580
  805.8 212.4 %slice-start.2 = ((s8[7372800]{0:T(1024)(128)(4,1)}), s8[4194304]{0:T(1024)(128)(4,1)S(1)}, s32[]{:S(2)}) async-start(s8[7372800]{0:T(1024)(128)(4,1)} %bitcast.329), calls=%async_computation.8 | async-start | bytes 8388608
  805.8 212.4 %slice-start.6 = ((s8[7372800]{0:T(1024)(128)(4,1)}), s8[4194304]{0:T(1024)(128)(4,1)S(1)}, s32[]{:S(2)}) async-start(s8[7372800]{0:T(1024)(128)(4,1)} %bitcast.333), calls=%async_computation.12 | async-start | bytes 8388608
  877.2 141.1 %slice-start.3 = ((s8[7372800]{0:T(1024)(128)(4,1)}), s8[3178496]{0:T(1024)(128)(4,1)S(1)}, s32[]{:S(2)}) async-start(s8[7372800]{0:T(1024)(128)(4,1)} %bitcast.329), calls=%async_computation.9 | async-start | bytes 6356992
  877.2 141.1 %slice-start.7 = ((s8[7372800]{0:T(1024)(128)(4,1)}), s8[3178496]{0:T(1024)(128)(4,1)S(1)}, s32[]{:S(2)}) async-start(s8[7372800]{0:T(1024)(128)(4,1)} %bitcast.333), calls=%async_computation.13 | async-start | bytes 6356992
  947.7 70.7 %copy-start.5 = (f32[30,30]{1,0:T(8,128)S(1)}, f32[30,30]{1,0:T(8,128)}, u32[]{:S(2)}) copy-start(f32[30,30]{1,0:T(8,128)} %copy-done.4) | copy-start | bytes 10804
  1018.3 15.2 %copy-start.7 = (f32[2048]{0:T(1024)S(1)}, f32[2048]{0:T(1024)}, u32[]{:S(2)}) copy-start(f32[2048]{0:T(1024)} %copy-done.6) | copy-start | bytes 24580
  1018.4 15.1 %copy-start.9 = (f32[2048]{0:T(1024)S(1)}, f32[2048]{0:T(1024)}, u32[]{:S(2)}) copy-start(f32[2048]{0:T(1024)} %copy-done.8) | copy-start | bytes 24580
  1018.4 15.1 %copy-start.11 = (f32[2048]{0:T(1024)S(1)}, f32[2048]{0:T(1024)}, u32[]{:S(2)}) copy-start(f32[2048]{0:T(1024)} %copy-done.10) | copy-start | bytes 24580
  1018.4 15.1 %copy-start.17 = (f32[30]{0:T(128)S(1)}, f32[30]{0:T(128)}, u32[]{:S(2)}) copy-start(f32[30]{0:T(128)} %copy-done.16) | copy-start | bytes 364
  1018.4 15.1 %copy-start.19 = (f32[30]{0:T(128)S(1)}, f32[30]{0:T(128)}, u32[]{:S(2)}) copy-start(f32[30]{0:T(128)} %copy-done.18) | copy-start | bytes 364
  1018.4 15.1 %copy-start.21 = (f32[30]{0:T(128)S(1)}, f32[30]{0:T(128)}, u32[]{:S(2)}) copy-start(f32[30]{0:T(128)} %copy-done.20) | copy-start | bytes 364
  1188.8 75.0 %copy-start.13 = (f32[2048]{0:T(1024)S(1)}, f32[2048]{0:T(1024)}, u32[]{:S(2)}) copy-start(f32[2048]{0:T(1024)} %get-tuple-element.49) | copy-start | bytes 24580
  1188.9 75.0 %copy-start.15 = (f32[2048]{0:T(1024)S(1)}, f32[2048]{0:T(1024)}, u32[]{:S(2)}) copy-start(f32[2048]{0:T(1024)} %get-tuple-element.50) | copy-start | bytes 24580
  1338.6 29.0 %copy-start.23 = (f32[30]{0:T(128)S(1)}, f32[30]{0:T(128)}, u32[]{:S(2)}) copy-start(f32[30]{0:T(128)} %param.7) | copy-start | bytes 364
where the time goes:
time: 1400 us; the launch traced here: 1390 us
  matrix products  1180 us (84%)
  blocking collectives  74.2 us (5%)
  local copies, waits for them, and re-layouts  58.3 us (4%)
  other arithmetic  57.4 us (4%)
  waiting for transfers between devices  14.9 us (1%)
    dot_general x8, matrix products, transform(): jnp.matmul(imag_part, sine, precision=HIGHEST)  297 us
    dot_general x8, matrix products, transform(): jnp.matmul(real_part, sine, precision=HIGHEST)  295 us
    dot_general x8, matrix products, transform(): jnp.matmul(imag_part, cosine, precision=HIGHEST)  294 us
    dot_general x8, matrix products, transform(): jnp.matmul(real_part, cosine, precision=HIGHEST)  292 us
    all_to_all x2, blocking collectives, per_device(): lax.all_to_all(moved, 'freq', split_axis=4, concat_axis=4, tiled=True)  38.8 us
  transfers between devices with their start and end apart: 2, of which 1 were waited for; matrix products, arithmetic and copies ran while one was open for 2% of the time, Pallas kernels for 0%

commit v1 on v0

--- a/solution.py
+++ b/solution.py
@@ -101,7 +101,12 @@
         moved = jnp.stack((real_part, imag_part), axis=1).reshape(evolve_rows.shape)
         columns = nonlinear_phase(
             transform(
-                lax.all_to_all(moved, "freq", split_axis=4, concat_axis=4, tiled=True),
+                jnp.concatenate(
+                    lax.all_to_all(
+                        jnp.stack(jnp.split(moved, lax.axis_size("freq"), axis=4)), "freq", 0, 0
+                    ),
+                    axis=4,
+                ),
                 inverse_short_cos,
                 inverse_short_sin,
             )

time: 1400 us -> 1620 us (1.16)
  local copies, waits for them, and re-layouts: 58.3 us -> 276 us
    split x0 -> x62, local copies, waits for them, and re-layouts: none -> 197 us  [per_device(): jnp.split(moved, lax.axis_size('freq'), axis=4)]
    unnamed x78 -> x142, local copies, waits for them, and re-layouts: 11.8 us -> 35.5 us
  transfers between devices with their start and end apart: 2 -> 2, of which waited for: 1 -> 1; matrix products, arithmetic and copies ran while one was open for 2% -> 1% of each run, Pallas kernels for 0% -> 0%
where the time goes in v1:
time: 1620 us; the launch traced here: 1610 us
  matrix products  1180 us (73%)
  local copies, waits for them, and re-layouts  276 us (17%)
  blocking collectives  74.6 us (5%)
  other arithmetic  54.6 us (3%)
    dot_general x8, matrix products, transform(): jnp.matmul(imag_part, sine, precision=HIGHEST)  296 us
    dot_general x8, matrix products, transform(): jnp.matmul(real_part, sine, precision=HIGHEST)  295 us
    dot_general x8, matrix products, transform(): jnp.matmul(imag_part, cosine, precision=HIGHEST)  294 us
    dot_general x8, matrix products, transform(): jnp.matmul(real_part, cosine, precision=HIGHEST)  292 us
    split x62, local copies, waits for them, and re-layouts, per_device(): jnp.split(moved, lax.axis_size('freq'), axis=4)  197 us
    all_to_all x2, blocking collectives, per_device(): lax.all_to_all(jnp.stack(jnp.split(moved, lax.axis_size('freq'), axis=4))...  39.1 us
    unnamed x142, local copies, waits for them, and re-layouts  35.5 us
  transfers between devices with their start and end apart: 2, of which 1 were waited for; matrix products, arithmetic and copies ran while one was open for 1% of the time, Pallas kernels for 0%

profile of v1, /device:TPU:0, one launch (start us, length us, event | category | flops | bytes accessed | tf_op | source)
XLA Modules:
  0.0 1610.0 jit_solution(1117517528023880022)
XLA Ops:
  4.6 7.3 all-to-all-start
  12.1 14.9 all-to-all-done
  36.1 3.1 all-to-all-start.1
  39.2 19.7 %fusion.352 = (f32[1,30,30,2048]{3,0,2,1:T(1,128)}, f32[1,30,30,2048]{3,0,2,1:T(1,128)}) fusion(f32[2,30,30,2048]{3,0,2,1:T(2,128)} %param.5), kind=kLoop, calls=%fused_computation.446 | loop fusion | bytes 29491200 | tf_op jit(solution)/shard_map/slice | solution.py:70
  65.2 71.2 %fusion.12 = f32[30,2048]{1,0:T(8,128)S(1)} fusion(f32[1,1,30,2048]{3,1,2,0:T(1,128)S(1)} %get-tuple-element.107), kind=kOutput, calls=%fused_computation.15 | convolution fusion | flops 1572864000 | bytes 491520 | tf_op jit(solution)/shard_map/dot_general | solution.py:23
  136.4 71.4 %fusion.10 = f32[30,2048]{1,0:T(8,128)S(1)} fusion(f32[1,1,30,2048]{3,1,2,0:T(1,128)S(1)} %get-tuple-element.108), kind=kOutput, calls=%fused_computation.13 | convolution fusion | flops 1572864000 | bytes 491520 | tf_op jit(solution)/shard_map/dot_general | solution.py:26
  207.8 70.6 %fusion.65 = f32[2048,30]{0,1:T(8,128)S(1)} fusion(f32[30,2048]{1,0:T(8,128)S(1)} %fusion.12, f32[1,1,30,2048]{3,1,2,0:T(1,128)S(1)} %get-tuple-element.108), kind=kOutput, calls=%fused_computation.52 | convolution fusion | flops 1568731136 | bytes 737280 | tf_op jit(solution)/shard_map/dot_general | solution.py:23
  278.4 70.4 %fusion.71 = f32[2048,30]{0,1:T(8,128)S(1)} fusion(f32[30,2048]{1,0:T(8,128)S(1)} %fusion.10, f32[1,1,30,2048]{3,1,2,0:T(1,128)S(1)} %get-tuple-element.107), kind=kOutput, calls=%fused_computation.54 | convolution fusion | flops 1568731136 | bytes 737280 | tf_op jit(solution)/shard_map/dot_general | solution.py:26
  348.9 11.7 multiply_reduce_fusion.6
  364.0 6.9 fusion.100
  370.9 74.2 %fusion.30 = f32[30,2048]{1,0:T(8,128)S(1)} fusion(f32[30,2048]{0,1:T(8,128)S(1)} %get-tuple-element.27), kind=kOutput, calls=%fused_computation.28 | convolution fusion | flops 1568669696 | bytes 491520 | tf_op jit(solution)/shard_map/dot_general | solution.py:23
  445.1 74.4 %fusion.28 = f32[30,2048]{1,0:T(8,128)S(1)} fusion(f32[1,30,2048]{1,2,0:T(8,128)S(1)} %get-tuple-element.28), kind=kOutput, calls=%fused_computation.27 | convolution fusion | flops 1568669696 | bytes 491520 | tf_op jit(solution)/shard_map/dot_general | solution.py:26
  519.6 74.7 %fusion.50 = f32[30,2048]{1,0:T(8,128)S(1)} fusion(f32[30,2048]{1,0:T(8,128)S(1)} %fusion.30, f32[1,30,2048]{1,2,0:T(8,128)S(1)} %get-tuple-element.28), kind=kOutput, calls=%fused_computation.47 | convolution fusion | flops 1568731136 | bytes 737280 | tf_op jit(solution)/shard_map/dot_general | solution.py:23
  594.4 75.0 %multiply_add_fusion.4 = (f32[30,2048]{1,0:T(8,128)S(1)}, f32[30,2048]{1,0:T(8,128)S(1)}) fusion(f32[30,2048]{1,0:T(8,128)S(1)} %fusion.50, f32[2048]{0:T(1024)S(1)} %copy-done.14, f32[2048]{0:T(1024)S(1)} %copy-done.12, f32[30,2048]{1,0:T(8,128)S(1)} %fusion.28, f32[30,2048]{0,1:T(8,128)S(1)} %get-tuple-element.27), kind=kOutput, calls=%fused_computation.157 | convolution fusion | flops 1569099776 | bytes 1245184 | tf_op jit(solution)/shard_map/dot_general | solution.py:26
  670.2 11.4 fusion.356
  681.5 15.4 fusion.355
  699.1 2.2 copy.3274
  703.6 2.8 copy.3272
  706.4 2.8 copy.3271
  709.2 2.8 copy.3270
  711.9 2.8 copy.3269
  714.7 2.8 copy.3268
  717.5 2.8 copy.3267
  720.3 2.8 copy.3266
  745.2 2.8 copy.3283
  748.0 2.8 copy.3282
  750.8 2.8 copy.3281
  753.6 2.8 copy.3280
  756.4 2.8 copy.3279
  759.2 2.8 copy.3278
  762.0 2.8 copy.3277
  764.8 2.8 copy.3276
  783.0 21.2 %all_to_all.30 = f32[32,1,3840]{2,1,0:T(1,128)S(1)} all-to-all(f32[32,1,3840]{2,1,0:T(1,128)S(1)} %reshape.919), channel_id=1, replica_groups=mesh['freq'=32] {'freq'}, dimensions={0} | all-to-all | bytes 983040 | tf_op jit(solution)/shard_map/all_to_all | solution.py:105
  813.0 2.5 convolution_add_fusion.1
  815.6 2.6 subtract_bitcast_fusion
  820.1 17.9 %all_to_all.31 = f32[32,1,3840]{2,1,0:T(1,128)S(1)} all-to-all(f32[32,1,3840]{2,1,0:T(1,128)S(1)} %reshape.921), channel_id=1, replica_groups=mesh['freq'=32] {'freq'}, dimensions={0} | all-to-all | bytes 983040 | tf_op jit(solution)/shard_map/all_to_all | solution.py:79
  842.7 71.2 %fusion.8 = f32[30,2048]{1,0:T(8,128)S(1)} fusion(f32[1,1,30,2048]{3,1,2,0:T(1,128)S(1)} %get-tuple-element.105), kind=kOutput, calls=%fused_computation.11 | convolution fusion | flops 1572864000 | bytes 491520 | tf_op jit(solution)/shard_map/dot_general | solution.py:23
  913.9 71.4 %fusion.6 = f32[30,2048]{1,0:T(8,128)S(1)} fusion(f32[1,1,30,2048]{3,1,2,0:T(1,128)S(1)} %get-tuple-element.106), kind=kOutput, calls=%fused_computation.9 | convolution fusion | flops 1572864000 | bytes 491520 | tf_op jit(solution)/shard_map/dot_general | solution.py:26
  985.3 70.6 %fusion.77 = f32[2048,30]{0,1:T(8,128)S(1)} fusion(f32[30,2048]{1,0:T(8,128)S(1)} %fusion.8, f32[1,1,30,2048]{3,1,2,0:T(1,128)S(1)} %get-tuple-element.106), kind=kOutput, calls=%fused_computation.56 | convolution fusion | flops 1568731136 | bytes 737280 | tf_op jit(solution)/shard_map/dot_general | solution.py:23
  1056.0 70.4 %fusion.83 = f32[2048,30]{0,1:T(8,128)S(1)} fusion(f32[30,2048]{1,0:T(8,128)S(1)} %fusion.6, f32[1,1,30,2048]{3,1,2,0:T(1,128)S(1)} %get-tuple-element.105), kind=kOutput, calls=%fused_computation.58 | convolution fusion | flops 1568731136 | bytes 737280 | tf_op jit(solution)/shard_map/dot_general | solution.py:26
  1126.5 11.7 multiply_reduce_fusion.2
  1141.6 6.9 fusion.95
  1148.5 74.2 %fusion.22 = f32[30,2048]{1,0:T(8,128)S(1)} fusion(f32[30,2048]{0,1:T(8,128)S(1)} %get-tuple-element.25), kind=kOutput, calls=%fused_computation.24 | convolution fusion | flops 1568669696 | bytes 491520 | tf_op jit(solution)/shard_map/dot_general | solution.py:23
  1222.7 74.4 %fusion.20 = f32[30,2048]{1,0:T(8,128)S(1)} fusion(f32[1,30,2048]{1,2,0:T(8,128)S(1)} %get-tuple-element.26), kind=kOutput, calls=%fused_computation.23 | convolution fusion | flops 1568669696 | bytes 491520 | tf_op jit(solution)/shard_map/dot_general | solution.py:26
  1297.2 74.7 %fusion.56 = f32[30,2048]{1,0:T(8,128)S(1)} fusion(f32[30,2048]{1,0:T(8,128)S(1)} %fusion.22, f32[1,30,2048]{1,2,0:T(8,128)S(1)} %get-tuple-element.26), kind=kOutput, calls=%fused_computation.49 | convolution fusion | flops 1568731136 | bytes 737280 | tf_op jit(solution)/shard_map/dot_general | solution.py:23
  1371.9 75.0 %multiply_add_fusion.3 = (f32[30,2048]{1,0:T(8,128)S(1)}, f32[30,2048]{1,0:T(8,128)S(1)}) fusion(f32[30,2048]{1,0:T(8,128)S(1)} %fusion.56, f32[2048]{0:T(1024)S(1)} %copy-done.15, f32[2048]{0:T(1024)S(1)} %copy-done.13, f32[30,2048]{1,0:T(8,128)S(1)} %fusion.20, f32[30,2048]{0,1:T(8,128)S(1)} %get-tuple-element.25), kind=kOutput, calls=%fused_computation.155 | convolution fusion | flops 1569099776 | bytes 1245184 | tf_op jit(solution)/shard_map/dot_general | solution.py:26
  1447.8 11.3 fusion.354
  1459.1 15.6 fusion.353
  1483.5 2.8 copy.3333
  1486.4 2.8 copy.3332
  1489.2 2.8 copy.3331
  1492.0 2.8 copy.3330
  1494.7 2.8 copy.3329
  1497.5 2.8 copy.3328
  1522.4 2.8 copy.3345
  1525.2 2.8 copy.3344
  1528.0 2.8 copy.3343
  1530.8 2.8 copy.3342
  1533.6 2.8 copy.3341
  1536.4 2.8 copy.3340
  1539.2 2.8 copy.3339
  1542.0 2.8 copy.3338
  1559.4 17.9 %all_to_all.32 = f32[32,1,3840]{2,1,0:T(1,128)S(1)} all-to-all(f32[32,1,3840]{2,1,0:T(1,128)S(1)} %reshape.923), channel_id=1, replica_groups=mesh['freq'=32] {'freq'}, dimensions={0} | all-to-all | bytes 983040 | tf_op jit(solution)/shard_map/all_to_all | solution.py:105
  1586.9 17.7 %all_to_all.33 = f32[32,1,3840]{2,1,0:T(1,128)S(1)} all-to-all(f32[32,1,3840]{2,1,0:T(1,128)S(1)} %reshape.925), channel_id=1, replica_groups=mesh['freq'=32] {'freq'}, dimensions={0} | all-to-all | bytes 983040 | tf_op jit(solution)/shard_map/all_to_all | solution.py:116
  (250 shorter events, 145.4 us)
Async XLA Ops:
  4.6 22.4 %all-to-all-start = ((f32[32,1,3840]{2,1,0:T(1,128)}), f32[32,1,3840]{2,1,0:T(1,128)S(1)}, u32[]{:S(2)}, u32[]{:S(2)}) async-start(f32[32,1,3840]{2,1,0:T(1,128)} %reshape.915), calls=%async_computation | async-start | bytes 983040 | tf_op jit(solution)/shard_map/all_to_all | solution.py:73
  12.1 46.9 %copy-start = (f32[64,32]{0,1:T(8,128)}, f32[64,32]{0,1:T(8,128)S(1)}, u32[]{:S(2)}) copy-start(f32[64,32]{0,1:T(8,128)S(1)} %get-tuple-element.112) | copy-start | bytes 24580
  12.1 46.9 %copy-start.2 = (f32[64,32]{0,1:T(8,128)}, f32[64,32]{0,1:T(8,128)S(1)}, u32[]{:S(2)}) copy-start(f32[64,32]{0,1:T(8,128)S(1)} %get-tuple-element.113) | copy-start | bytes 24580
  36.1 24.2 %all-to-all-start.1 = ((f32[32,1,3840]{2,1,0:T(1,128)}), f32[32,1,3840]{2,1,0:T(1,128)S(1)}, u32[]{:S(2)}, u32[]{:S(2)}) async-start(f32[32,1,3840]{2,1,0:T(1,128)} %reshape.917), calls=%async_computation.1 | async-start | bytes 983040 | tf_op jit(solution)/shard_map/all_to_all | solution.py:79
  39.2 21.1 %copy-start.24 = (f32[3,30]{1,0:T(4,128)S(1)}, f32[3,30]{1,0:T(4,128)}, u32[]{:S(2)}) copy-start(f32[3,30]{1,0:T(4,128)} %param.6) | copy-start | bytes 1084
  59.0 305.0 %copy-start.6 = (f32[2048]{0:T(1024)}, f32[2048]{0:T(1024)S(1)}, u32[]{:S(2)}) copy-start(f32[2048]{0:T(1024)S(1)} %fusion.210) | copy-start | bytes 24580
  59.0 289.8 %copy-start.4 = (f32[30,30]{1,0:T(8,128)}, f32[30,30]{1,0:T(8,128)S(1)}, u32[]{:S(2)}) copy-start(f32[30,30]{1,0:T(8,128)S(1)} %fusion.171) | copy-start | bytes 10804
  59.7 304.3 %copy-start.8 = (f32[2048]{0:T(1024)}, f32[2048]{0:T(1024)S(1)}, u32[]{:S(2)}) copy-start(f32[2048]{0:T(1024)S(1)} %get-tuple-element.117) | copy-start | bytes 24580
  60.3 303.6 %copy-start.10 = (f32[2048]{0:T(1024)}, f32[2048]{0:T(1024)S(1)}, u32[]{:S(2)}) copy-start(f32[2048]{0:T(1024)S(1)} %get-tuple-element.114) | copy-start | bytes 24580
  60.3 303.6 %copy-start.16 = (f32[30]{0:T(128)}, f32[30]{0:T(128)S(1)}, u32[]{:S(2)}) copy-start(f32[30]{0:T(128)S(1)} %get-tuple-element.109) | copy-start | bytes 364
  60.4 303.6 %copy-start.18 = (f32[30]{0:T(128)}, f32[30]{0:T(128)S(1)}, u32[]{:S(2)}) copy-start(f32[30]{0:T(128)S(1)} %get-tuple-element.110) | copy-start | bytes 364
  60.4 303.6 %copy-start.20 = (f32[30]{0:T(128)}, f32[30]{0:T(128)S(1)}, u32[]{:S(2)}) copy-start(f32[30]{0:T(128)S(1)} %get-tuple-element.111) | copy-start | bytes 364
  207.8 141.0 %slice-start = ((s8[7372800]{0:T(1024)(128)(4,1)}), s8[4194304]{0:T(1024)(128)(4,1)S(1)}, s32[]{:S(2)}) async-start(s8[7372800]{0:T(1024)(128)(4,1)} %bitcast.415), calls=%async_computation.6 | async-start | bytes 8388608
  207.8 141.0 %slice-start.4 = ((s8[7372800]{0:T(1024)(128)(4,1)}), s8[4194304]{0:T(1024)(128)(4,1)S(1)}, s32[]{:S(2)}) async-start(s8[7372800]{0:T(1024)(128)(4,1)} %bitcast.419), calls=%async_computation.10 | async-start | bytes 8388608
  278.4 70.4 %slice-start.1 = ((s8[7372800]{0:T(1024)(128)(4,1)}), s8[3178496]{0:T(1024)(128)(4,1)S(1)}, s32[]{:S(2)}) async-start(s8[7372800]{0:T(1024)(128)(4,1)} %bitcast.415), calls=%async_computation.7 | async-start | bytes 6356992
  278.4 70.4 %slice-start.5 = ((s8[7372800]{0:T(1024)(128)(4,1)}), s8[3178496]{0:T(1024)(128)(4,1)S(1)}, s32[]{:S(2)}) async-start(s8[7372800]{0:T(1024)(128)(4,1)} %bitcast.419), calls=%async_computation.11 | async-start | bytes 6356992
  519.6 74.8 %copy-start.12 = (f32[2048]{0:T(1024)S(1)}, f32[2048]{0:T(1024)}, u32[]{:S(2)}) copy-start(f32[2048]{0:T(1024)} %get-tuple-element.116) | copy-start | bytes 24580
  519.6 74.8 %copy-start.14 = (f32[2048]{0:T(1024)S(1)}, f32[2048]{0:T(1024)}, u32[]{:S(2)}) copy-start(f32[2048]{0:T(1024)} %get-tuple-element.115) | copy-start | bytes 24580
  759.2 50.4 %copy-start.22 = (f32[30]{0:T(128)S(1)}, f32[30]{0:T(128)}, u32[]{:S(2)}) copy-start(f32[30]{0:T(128)} %param.7) | copy-start | bytes 364
  764.8 50.7 %copy-start.1 = (f32[64,32]{0,1:T(8,128)S(1)}, f32[64,32]{0,1:T(8,128)}, u32[]{:S(2)}) copy-start(f32[64,32]{0,1:T(8,128)} %copy-done) | copy-start | bytes 24580
  764.8 50.7 %copy-start.3 = (f32[64,32]{0,1:T(8,128)S(1)}, f32[64,32]{0,1:T(8,128)}, u32[]{:S(2)}) copy-start(f32[64,32]{0,1:T(8,128)} %copy-done.2) | copy-start | bytes 24580
  985.3 141.0 %slice-start.2 = ((s8[7372800]{0:T(1024)(128)(4,1)}), s8[4194304]{0:T(1024)(128)(4,1)S(1)}, s32[]{:S(2)}) async-start(s8[7372800]{0:T(1024)(128)(4,1)} %bitcast.417), calls=%async_computation.8 | async-start | bytes 8388608
  985.3 141.0 %slice-start.6 = ((s8[7372800]{0:T(1024)(128)(4,1)}), s8[4194304]{0:T(1024)(128)(4,1)S(1)}, s32[]{:S(2)}) async-start(s8[7372800]{0:T(1024)(128)(4,1)} %bitcast.421), calls=%async_computation.12 | async-start | bytes 8388608
  1055.9 70.4 %slice-start.3 = ((s8[7372800]{0:T(1024)(128)(4,1)}), s8[3178496]{0:T(1024)(128)(4,1)S(1)}, s32[]{:S(2)}) async-start(s8[7372800]{0:T(1024)(128)(4,1)} %bitcast.417), calls=%async_computation.9 | async-start | bytes 6356992
  1056.0 70.4 %slice-start.7 = ((s8[7372800]{0:T(1024)(128)(4,1)}), s8[3178496]{0:T(1024)(128)(4,1)S(1)}, s32[]{:S(2)}) async-start(s8[7372800]{0:T(1024)(128)(4,1)} %bitcast.421), calls=%async_computation.13 | async-start | bytes 6356992
  1056.0 70.4 %copy-start.5 = (f32[30,30]{1,0:T(8,128)S(1)}, f32[30,30]{1,0:T(8,128)}, u32[]{:S(2)}) copy-start(f32[30,30]{1,0:T(8,128)} %copy-done.4) | copy-start | bytes 10804
  1126.4 15.2 copy-start.7
  1126.4 15.2 copy-start.9
  1126.4 15.2 copy-start.11
  1126.4 15.1 copy-start.17
  1126.4 15.1 copy-start.19
  1126.5 15.1 copy-start.21
  1297.2 74.8 %copy-start.13 = (f32[2048]{0:T(1024)S(1)}, f32[2048]{0:T(1024)}, u32[]{:S(2)}) copy-start(f32[2048]{0:T(1024)} %get-tuple-element.116) | copy-start | bytes 24580
  1297.2 74.8 %copy-start.15 = (f32[2048]{0:T(1024)S(1)}, f32[2048]{0:T(1024)}, u32[]{:S(2)}) copy-start(f32[2048]{0:T(1024)} %get-tuple-element.115) | copy-start | bytes 24580
  1536.4 46.4 %copy-start.23 = (f32[30]{0:T(128)S(1)}, f32[30]{0:T(128)}, u32[]{:S(2)}) copy-start(f32[30]{0:T(128)} %param.7) | copy-start | bytes 364
